TPU v7x, 32 devices: a whole 2x2x4 slice. The times are simulated.
32 devices in a mesh: gx: 2 (over x), gy: 16 (over z, y, core).
Axes of the slice: x: 2, y: 2, z: 4, core: 2. Of those that a mesh axis runs over, the one named last changes fastest.
Arguments:
- trial: float32 [49152, 384], P(('gx', 'gy')), may hold values from -30 to 30
- resid: float32 [49152, 128], P(('gx', 'gy')), may hold values from -500 to 500
- energy: float32 [49152], P(('gx', 'gy')), may hold values from 1 to 10
- shift: float32 [128], replicated, may hold values from 0.05 to 0.5
Outputs:
- basis: float32 [49152, 128], P(('gx', 'gy'))
All inputs are finite; a program needn't handle non-finite values.
Results may differ from a plain program's by a relative error of at most 0.0003.
Values sent between devices are 32-bit elements; how exact they have to be, the bound alone decides.
A program may use at most 64 MiB of HBM per device.

v0:
```python
import functools

import jax
import jax.numpy as jnp
from jax import lax
from jax.experimental import pallas as pl
from jax.experimental.pallas import tpu as pltpu
from jax.sharding import PartitionSpec as P

MESH = pl.DeviceIdType.MESH
LANES = 128
HALF = LANES // 2


def bdot(left, right, dims):
    return lax.dot_general(left, right, (dims, ((), ())), preferred_element_type=jnp.float32)


def chunk_rows(total, owners):
    return -(-total // (8 * owners)) * 8


def ranges(count, step):
    return [(start, min(step, count - start)) for start in range(0, count, step)]


def split(values):
    high = values.astype(jnp.bfloat16)
    rest = values - high.astype(jnp.float32)
    middle = rest.astype(jnp.bfloat16)
    low = (rest - middle.astype(jnp.float32)).astype(jnp.bfloat16)
    return high, middle, low


def dot(left, right, dims):
    return lax.dot_general(
        left, right, (dims, ((), ())),
        precision=lax.Precision.HIGHEST, preferred_element_type=jnp.float32,
    )


def wide(high, middle, low, right):
    a, b, c = split(right)
    both = jnp.concatenate([a, b], axis=1)
    width = right.shape[1]
    one = bdot(high, both, ((1,), (0,)))
    two = bdot(middle, both, ((1,), (0,)))
    rest = bdot(high, c, ((1,), (0,))) + bdot(low, a, ((1,), (0,)))
    return one[:, :width] + (one[:, width:] + two[:, :width] + (rest + two[:, width:]))


def outer(left, right):
    a, b, c = split(left)
    d, e, f = split(right)
    return lax.dot_general(
        jnp.concatenate([a, a, b, b, a, c], 0), jnp.concatenate([d, e, d, e, f, d], 0),
        (((0,), (0,)), ((), ())), preferred_element_type=jnp.float32)


def inverse_factor(square, width):
    size = square.shape[0]
    row = lax.broadcasted_iota(jnp.int32, (size, size), 0)
    col = lax.broadcasted_iota(jnp.int32, (size, size), 1)
    both = jnp.concatenate([square, (row == col).astype(jnp.float32)], axis=1)
    local = lax.broadcasted_iota(jnp.int32, (width, size), 0)
    out = []
    for start in range(0, size, width):
        slab, side = both[:width, :size], both[:width, size:]
        cols = [jnp.broadcast_to(slab[:, start + j:start + j + 1], (width, size)) for j in range(width)]
        scale = jnp.ones((width, size), jnp.float32)
        for j in range(width):
            inverse = 1.0 / cols[j][j:j + 1, :]
            factor = jnp.where(local > j, cols[j] * inverse, 0.0)
            scale = jnp.where(local == j, inverse, scale)
            for m in range(j + 1, width):
                cols[m] = cols[m] - factor * cols[m][j:j + 1, :]
            slab = slab - factor * slab[j:j + 1, :]
            side = side - factor * side[j:j + 1, :]
        out.append(side * jnp.sqrt(scale))
        if start + width < size:
            update = outer(slab * scale, jnp.concatenate([slab, side], axis=1))
            both = both[width:] - update[start + width:]
    return jnp.concatenate(out, axis=0)


def kernel(
    nx, ny, count, trial, resid, energy, shift, basis,
    xs, xh, xm, xl, wh, wm, wl, held, load, load_resid, gram, part, swap, acc, landed, red, full, gpart, glanded, gred,
    swap_send, swap_recv, rs_send, rs_recv, ag_send, ag_recv, fw_send, fw_recv,
    gs_send, gs_recv, ga_send, ga_recv,
):
    ix, iy = lax.axis_index("gx"), lax.axis_index("gy")
    pairs_y = ny // 2
    np_ = nx * pairs_y
    ndev = nx * ny
    me, core = ix * pairs_y + iy // 2, iy % 2
    flat = me * 2 + core
    kept = trial.shape[1]
    keep = kept // LANES
    fetch = pltpu.make_async_copy(trial, xs.at[:, pl.ds(0, kept)], load)
    fetch.start()
    fetch_resid = pltpu.make_async_copy(resid, held, load_resid)
    fetch_resid.start()
    rows = trial.shape[0]
    half = acc.shape[0]
    rs_rows = red.shape[0]
    owners = half // rs_rows
    g_rows = gred.shape[0]
    g_owners = LANES // g_rows

    def where(pair, which):
        return (pair // pairs_y, (pair % pairs_y) * 2 + which)

    def others(total, mine, body):
        def step(k, carry):
            body(lax.rem(mine + k, total))
            return carry
        lax.fori_loop(1, total, step, 0)

    barrier = pltpu.get_barrier_semaphore()

    def greet(other):
        pl.semaphore_signal(barrier, inc=1, device_id=where(other // 2, other % 2), device_id_type=MESH)
    others(ndev, flat, greet)

    fetch_resid.wait()
    for block in range(rows // LANES):
        span = pl.ds(block * LANES, LANES)
        level = jnp.broadcast_to(energy[block:block + 1, :], (LANES, LANES)).T
        xs[span, kept:] = held[span, :] / (level - shift[...])
    fetch.wait()
    for start, size in ranges(rows, LANES):
        span = pl.ds(start, size)
        xh[span, :], xm[span, :], xl[span, :] = split(xs[span, :])

    slots = {}
    spans = []
    for i in range(keep):
        first_place = len(slots)
        for j in range(i, keep):
            slots[i, j] = len(slots)
        slots["r", i] = len(slots)
        spans.append((first_place * HALF, len(slots) * HALF))

    def stripe(i):
        left, right = pl.ds(i * LANES, LANES), slice(i * LANES, None)
        total = None
        for one, two in ((xm, xm), (xl, xh), (xh, xl), (xm, xh), (xh, xm), (xh, xh)):
            term = bdot(one[:, left], two[:, right], ((0,), (0,)))
            total = term if total is None else total + term
        for j in range(keep - i + 1):
            start = spans[i][0] + j * HALF
            for which in range(2):
                part[pl.ds(which * half + start, HALF), :] = total[
                    which * HALF:(which + 1) * HALF, j * LANES:(j + 1) * LANES]

    def read(name):
        return jnp.concatenate(
            [full[pl.ds(which * half + slots[name] * HALF, HALF), :] for which in range(2)], axis=0)

    def rows_of(index, size, base=0):
        return pl.ds(pl.multiple_of(base + index * size, 8), size)

    def exchange(i):
        low, high = spans[i]
        return pltpu.make_async_remote_copy(
            src_ref=part.at[pl.ds(pl.multiple_of((1 - core) * half + low, 8), high - low)],
            dst_ref=swap.at[pl.ds(low, high - low)],
            send_sem=swap_send.at[i], recv_sem=swap_recv.at[i],
            device_id=where(me, 1 - core), device_id_type=MESH)

    def scatter(other):
        return pltpu.make_async_remote_copy(
            src_ref=acc.at[rows_of(other, rs_rows)], dst_ref=landed.at[me],
            send_sem=rs_send.at[other], recv_sem=rs_recv.at[me],
            device_id=where(other, core), device_id_type=MESH)

    def scatter_in(other):
        return pltpu.make_async_remote_copy(
            src_ref=acc.at[rows_of(0, rs_rows)], dst_ref=landed.at[other],
            send_sem=rs_send.at[other], recv_sem=rs_recv.at[other],
            device_id=where(other, core), device_id_type=MESH)

    def guarded(limit, body):
        def run(other):
            if limit >= np_:
                body(other)
            else:
                @pl.when(other < limit)
                def _():
                    body(other)
        return run

    sent = [0]

    def absorb(i):
        low, high = spans[i]
        exchange(i).wait_recv()
        acc[pl.ds(low, high - low), :] = (
            part[pl.ds(pl.multiple_of(core * half + low, 8), high - low), :] + swap[pl.ds(low, high - low), :])
        begin, end = sent[0], owners if i == keep - 1 else high // rs_rows
        sent[0] = end

        def send(k, carry):
            other = begin + lax.rem(me + k, end - begin)

            @pl.when(other != me)
            def _():
                scatter(other).start()
            return carry
        lax.fori_loop(0, end - begin, send, 0)

    if spans[-1][1] < half:
        acc[pl.ds(spans[-1][1], half - spans[-1][1]), :] = jnp.zeros((half - spans[-1][1], LANES), jnp.float32)
    for i in range(keep):
        stripe(i)
        if i == 0:
            pl.semaphore_wait(barrier, ndev - 1)
        exchange(i).start()
        if i > 0:
            absorb(i - 1)
    absorb(keep - 1)

    base = core * half

    def gather(other):
        return pltpu.make_async_remote_copy(
            src_ref=red, dst_ref=full.at[rows_of(me, rs_rows, base)],
            send_sem=ag_send.at[other], recv_sem=ag_recv.at[me],
            device_id=where(other, core), device_id_type=MESH)

    def gather_in(other):
        return pltpu.make_async_remote_copy(
            src_ref=red, dst_ref=full.at[rows_of(other, rs_rows, base)],
            send_sem=ag_send.at[other], recv_sem=ag_recv.at[other],
            device_id=where(other, core), device_id_type=MESH)

    def forward(owner, source):
        return pltpu.make_async_remote_copy(
            src_ref=source, dst_ref=full.at[rows_of(owner, rs_rows, base)],
            send_sem=fw_send.at[owner], recv_sem=fw_recv.at[owner],
            device_id=where(me, 1 - core), device_id_type=MESH)

    def forward_in(owner):
        return pltpu.make_async_remote_copy(
            src_ref=red, dst_ref=full.at[rows_of(owner, rs_rows, half - base)],
            send_sem=fw_send.at[owner], recv_sem=fw_recv.at[owner],
            device_id=where(me, 1 - core), device_id_type=MESH)

    @pl.when(me < owners)
    def _():
        others(np_, me, lambda other: scatter_in(other).wait_recv())
        landed[me] = acc[rows_of(me, rs_rows), :]
        red[...] = lax.fori_loop(0, np_, lambda k, total: total + landed[k], jnp.zeros(red.shape, jnp.float32))
        others(np_, me, lambda other: gather(other).start())
        forward(me, red).start()
        full[rows_of(me, rs_rows, base), :] = red[...]

    def relay(other):
        gather_in(other).wait_recv()
        forward(other, full.at[rows_of(other, rs_rows, base)]).start()
    others(np_, me, guarded(owners, relay))
    lax.fori_loop(0, owners, lambda k, carry: (forward_in(k).wait_recv(), carry)[1], 0)

    raw = [read(("r", i)) for i in range(keep)]
    first = [one / count for one in raw]
    total = []
    for i in range(keep):
        metric = None
        for j in range(keep):
            block = read((min(i, j), max(i, j)))
            term = dot(block, first[j], ((1,), (0,)) if i <= j else ((0,), (0,)))
            metric = term if metric is None else metric + term
        total.append(first[i] + (raw[i] - metric) / count)
    coef = jnp.concatenate(total, axis=0)
    for start, size in ranges(rows, 256):
        span = pl.ds(start, size)
        block = xs[span, kept:] - wide(xh[span, :kept], xm[span, :kept], xl[span, :kept], coef)
        wh[span, :], wm[span, :], wl[span, :] = split(block)
    ours = wh[...]
    high = bdot(ours, ours, ((0,), (0,)))
    cross = bdot(ours, wm[...], ((0,), (0,))) + bdot(ours, wl[...], ((0,), (0,)))
    gpart[...] = high + (cross + cross.T + bdot(wm[...], wm[...], ((0,), (0,))))

    def gscatter(other):
        return pltpu.make_async_remote_copy(
            src_ref=gpart.at[rows_of(other, g_rows)], dst_ref=glanded.at[flat],
            send_sem=gs_send.at[other], recv_sem=gs_recv.at[flat],
            device_id=where(other, 0), device_id_type=MESH)

    def gscatter_in(other):
        return pltpu.make_async_remote_copy(
            src_ref=gpart.at[rows_of(0, g_rows)], dst_ref=glanded.at[other],
            send_sem=gs_send.at[0], recv_sem=gs_recv.at[other],
            device_id=where(other // 2, other % 2), device_id_type=MESH)

    def ggather(other):
        return pltpu.make_async_remote_copy(
            src_ref=gred, dst_ref=gram.at[rows_of(me, g_rows)],
            send_sem=ga_send.at[other], recv_sem=ga_recv.at[me],
            device_id=where(other // 2, other % 2), device_id_type=MESH)

    def ggather_in(owner):
        return pltpu.make_async_remote_copy(
            src_ref=gred, dst_ref=gram.at[rows_of(owner, g_rows)],
            send_sem=ga_send.at[0], recv_sem=ga_recv.at[owner],
            device_id=where(owner, 0), device_id_type=MESH)

    others(np_, me, guarded(g_owners, lambda other: gscatter(other).start()))

    @pl.when(jnp.logical_and(core == 1, me < g_owners))
    def _():
        gscatter(me).start()

    for i in range(keep):
        exchange(i).wait_send()
    others(np_, me, guarded(owners, lambda other: scatter(other).wait_send()))

    @pl.when(me < owners)
    def _():
        others(np_, me, lambda other: gather(other).wait_send())
    lax.fori_loop(0, owners, lambda k, carry: (forward_in(k).wait_send(), carry)[1], 0)
    others(np_, me, guarded(g_owners, lambda other: gscatter(other).wait_send()))

    @pl.when(jnp.logical_and(core == 1, me < g_owners))
    def _():
        gscatter(me).wait_send()

    @pl.when(jnp.logical_and(core == 0, me < g_owners))
    def _():
        others(ndev, flat, lambda other: gscatter_in(other).wait_recv())
        glanded[flat] = gpart[rows_of(me, g_rows), :]
        gred[...] = lax.fori_loop(
            0, ndev, lambda k, total: total + glanded[k], jnp.zeros(gred.shape, jnp.float32)) / count
        others(ndev, flat, lambda other: ggather(other).start())
        gram[rows_of(me, g_rows), :] = gred[...]

    others(np_, me, guarded(g_owners, lambda other: ggather_in(other).wait_recv()))

    @pl.when(jnp.logical_and(core == 1, me < g_owners))
    def _():
        ggather_in(me).wait_recv()

    inverse = inverse_factor(gram[...], 16).T
    for start, size in ranges(rows, 256):
        span = pl.ds(start, size)
        basis[span, :] = wide(wh[span, :], wm[span, :], wl[span, :], inverse)

    @pl.when(jnp.logical_and(core == 0, me < g_owners))
    def _():
        others(ndev, flat, lambda other: ggather(other).wait_send())


def per_device(nx, ny, trial, resid, energy, shift):
    rows, kept = trial.shape
    new = resid.shape[1]
    keep = kept // LANES
    blocks = keep + keep * (keep + 1) // 2
    np_ = nx * (ny // 2)
    rs_rows = chunk_rows(blocks * HALF, np_)
    owners = -(-blocks * HALF // rs_rows)
    half = owners * rs_rows
    g_rows = chunk_rows(LANES, np_)
    f32 = jnp.float32
    dma = pltpu.SemaphoreType.DMA
    vmem = pl.BlockSpec(memory_space=pltpu.VMEM)
    return pl.pallas_call(
        functools.partial(kernel, nx, ny, float(rows * nx * ny)),
        name="project",
        out_shape=jax.ShapeDtypeStruct((rows, new), f32),
        in_specs=[pl.BlockSpec(memory_space=pl.ANY)] * 2 + [vmem] * 2,
        out_specs=vmem,
        scratch_shapes=[
            pltpu.VMEM((rows, kept + new), f32),
            *[pltpu.VMEM((rows, kept + new), jnp.bfloat16)] * 3,
            *[pltpu.VMEM((rows, new), jnp.bfloat16)] * 3,
            pltpu.VMEM((rows, new), f32),
            dma, dma,
            pltpu.VMEM((new, new), f32),
            pltpu.VMEM((2 * half, LANES), f32),
            pltpu.VMEM((half, LANES), f32),
            pltpu.VMEM((half, LANES), f32),
            pltpu.VMEM((np_, rs_rows, LANES), f32),
            pltpu.VMEM((rs_rows, LANES), f32),
            pltpu.VMEM((2 * half, LANES), f32),
            pltpu.VMEM((LANES, LANES), f32),
            pltpu.VMEM((nx * ny, g_rows, LANES), f32),
            pltpu.VMEM((g_rows, LANES), f32),
            dma((keep,)), dma((keep,)), dma((np_,)), dma((np_,)), dma((np_,)), dma((np_,)), dma((owners,)), dma((owners,)),
            dma((np_,)), dma((nx * ny,)), dma((nx * ny,)), dma((np_,)),
        ],
        compiler_params=pltpu.CompilerParams(collective_id=0, has_side_effects=True),
    )(trial, resid, energy.reshape(rows // LANES, LANES), shift.reshape(1, new))


def solution(mesh):
    in_specs = (P(("gx", "gy"), None), P(("gx", "gy"), None), P(("gx", "gy")), P())
    out_specs = P(("gx", "gy"), None)
    body = functools.partial(per_device, mesh.shape["gx"], mesh.shape["gy"])
    return jax.shard_map(body, mesh=mesh, in_specs=in_specs, out_specs=out_specs, check_vma=False)
```

profile of v0, /device:TPU:0, one launch (start us, length us, event | category | flops | bytes accessed | tf_op | source)
XLA Modules:
  0.0 50.4 jit_solution(7287419175115673605)
XLA Ops:
  0.0 48.4 %project.1 = f32[1536,128]{1,0:T(8,128)} custom-call(f32[1536,384]{1,0:T(8,128)} %trial.1, f32[1536,128]{1,0:T(8,128)} %resid.1, f32[12,128]{1,0:T(8,128)} %bitcast.2, f32[1,128]{1,0:T(1,128)} %bitcast.3), custom_call_target="tpu_custom_call" | custom-call | tf_op jit(solution)/shard_map/project/pallas_call | solution.py:367
  48.4 2.1 %copy.6 = f32[1536,128]{1,0:T(8,128)} copy(f32[1536,128]{1,0:T(8,128)} %project.1) | data formatting | bytes 1572864
where the time goes:
time: 50.7 us; the launch traced here: 50.4 us
  Pallas kernels  48.4 us (95%)
  local copies, waits for them, and re-layouts  2.06 us (4%)
    pallas_call x1, Pallas kernels, per_device(): pl.pallas_call(functools.partial(kernel, nx, ny, float(rows * nx * ny)),...  48.4 us
    unnamed x1, local copies, waits for them, and re-layouts  2.06 us

commit v1 on v0

--- a/solution.py
+++ b/solution.py
@@ -10,6 +10,9 @@
 MESH = pl.DeviceIdType.MESH
 LANES = 128
 HALF = LANES // 2
+ROWS = 256
+SHARE_LIMIT = 32.0
+LENGTH_LIMIT = 1024.0
 
 
 def bdot(left, right, dims):
@@ -63,7 +66,7 @@
     col = lax.broadcasted_iota(jnp.int32, (size, size), 1)
     both = jnp.concatenate([square, (row == col).astype(jnp.float32)], axis=1)
     local = lax.broadcasted_iota(jnp.int32, (width, size), 0)
-    out = []
+    out, scales = [], []
     for start in range(0, size, width):
         slab, side = both[:width, :size], both[:width, size:]
         cols = [jnp.broadcast_to(slab[:, start + j:start + j + 1], (width, size)) for j in range(width)]
@@ -77,13 +80,14 @@
             slab = slab - factor * slab[j:j + 1, :]
             side = side - factor * side[j:j + 1, :]
         out.append(side * jnp.sqrt(scale))
+        scales.append(scale)
         if start + width < size:
             update = outer(slab * scale, jnp.concatenate([slab, side], axis=1))
             both = both[width:] - update[start + width:]
-    return jnp.concatenate(out, axis=0)
-
-
-def kernel(
+    return jnp.concatenate(out, axis=0), jnp.concatenate(scales, axis=0)
+
+
+def robust_kernel(
     nx, ny, count, trial, resid, energy, shift, basis,
     xs, xh, xm, xl, wh, wm, wl, held, load, load_resid, gram, part, swap, acc, landed, red, full, gpart, glanded, gred,
     swap_send, swap_recv, rs_send, rs_recv, ag_send, ag_recv, fw_send, fw_recv,
@@ -341,7 +345,7 @@
     def _():
         ggather_in(me).wait_recv()
 
-    inverse = inverse_factor(gram[...], 16).T
+    inverse = inverse_factor(gram[...], 16)[0].T
     for start, size in ranges(rows, 256):
         span = pl.ds(start, size)
         basis[span, :] = wide(wh[span, :], wm[span, :], wl[span, :], inverse)
@@ -351,7 +355,7 @@
         others(ndev, flat, lambda other: ggather(other).wait_send())
 
 
-def per_device(nx, ny, trial, resid, energy, shift):
+def robust_call(nx, ny, trial, resid, energy, shift):
     rows, kept = trial.shape
     new = resid.shape[1]
     keep = kept // LANES
@@ -365,8 +369,8 @@
     dma = pltpu.SemaphoreType.DMA
     vmem = pl.BlockSpec(memory_space=pltpu.VMEM)
     return pl.pallas_call(
-        functools.partial(kernel, nx, ny, float(rows * nx * ny)),
-        name="project",
+        functools.partial(robust_kernel, nx, ny, float(rows * nx * ny)),
+        name="robust",
         out_shape=jax.ShapeDtypeStruct((rows, new), f32),
         in_specs=[pl.BlockSpec(memory_space=pl.ANY)] * 2 + [vmem] * 2,
         out_specs=vmem,
@@ -389,8 +393,411 @@
             dma((keep,)), dma((keep,)), dma((np_,)), dma((np_,)), dma((np_,)), dma((np_,)), dma((owners,)), dma((owners,)),
             dma((np_,)), dma((nx * ny,)), dma((nx * ny,)), dma((np_,)),
         ],
+        compiler_params=pltpu.CompilerParams(collective_id=1, has_side_effects=True),
+    )(trial, resid, energy, shift)
+
+
+def halves(values):
+    high = values.astype(jnp.bfloat16)
+    return high, (values - high.astype(jnp.float32)).astype(jnp.bfloat16)
+
+
+def dot3(left, right):
+    a, b = left
+    c, d = right
+    width = c.shape[1]
+    one = bdot(a, jnp.concatenate([c, d], axis=1), ((1,), (0,)))
+    return one[:, :width] + (one[:, width:] + bdot(b, c, ((1,), (0,))))
+
+
+def plan(kept, new, owners):
+    blocks = (kept + new) // LANES
+    names, late = [], []
+    for i in range(0, blocks, 2):
+        pair = [(i, i)] + ([(i + 1, i + 1)] if i + 1 < blocks else [])
+        (names if i == 0 else late).append(("pack", *[p[0] for p in pair]))
+    for i in range(blocks):
+        for j in range(i + 1, blocks):
+            (names if i == 0 else late).append((i, j))
+    parts = []
+    start = 0
+    for group in (names, late):
+        rows = -(-len(group) * HALF // (8 * owners)) * 8 * owners
+        parts.append((group, start, rows))
+        start += rows
+    return parts, start, start + 8
+
+
+def reduce_kernel(
+    nx, ny, count, trial, resid, energy, shift, high_out, low_out, last_out, safe,
+    xs, xh, xm, held, load, load_resid, part, swap, acc, landed, landed_tail, red, red_tail, full,
+    swap_send, swap_recv, rs_send, rs_recv, ag_send, ag_recv, fw_send, fw_recv,
+):
+    ix, iy = lax.axis_index("gx"), lax.axis_index("gy")
+    pairs_y = ny // 2
+    np_ = nx * pairs_y
+    ndev = nx * ny
+    me, core = ix * pairs_y + iy // 2, iy % 2
+    flat = me * 2 + core
+    rows, kept = trial.shape
+    new = resid.shape[1]
+    keep = kept // LANES
+    blocks = keep + 1
+    groups, tail, half = plan(kept, new, np_)
+    center = np_ // 4
+    fetch_resid = pltpu.make_async_copy(resid, held, load_resid)
+    fetch_resid.start()
+    fetch = pltpu.make_async_copy(trial, xs, load)
+    fetch.start()
+
+    def where(pair, which):
+        return (pair // pairs_y, (pair % pairs_y) * 2 + which)
+
+    def others(total, mine, body):
+        def step(k, carry):
+            body(lax.rem(mine + 1 + lax.rem(k + total // 4, total - 1), total))
+            return carry
+        lax.fori_loop(0, total - 1, step, 0)
+
+    barrier = pltpu.get_barrier_semaphore()
+
+    def greet(other):
+        pl.semaphore_signal(barrier, inc=1, device_id=where(other // 2, other % 2), device_id_type=MESH)
+    others(ndev, flat, greet)
+
+    with jax.named_scope("corr"):
+        fetch_resid.wait()
+        for block in range(rows // LANES):
+            span = pl.ds(block * LANES, LANES)
+            level = jnp.broadcast_to(energy[block:block + 1, :], (LANES, LANES)).T
+            corr = held[span, :] / (level - shift[...])
+            held[span, :] = corr
+            xh[span, kept:], xm[span, kept:] = halves(corr)
+    with jax.named_scope("fetchsplit"):
+        fetch.wait()
+        for start, size in ranges(rows, LANES):
+            span = pl.ds(start, size)
+            xh[span, :kept], xm[span, :kept] = halves(xs[span, :])
+
+    row = lax.broadcasted_iota(jnp.int32, (LANES, LANES), 0)
+    col = lax.broadcasted_iota(jnp.int32, (LANES, LANES), 1)
+
+    def save(start, value):
+        size = value.shape[0] // 2
+        for which in range(2):
+            part[pl.ds(which * half + start, size), :] = value[which * size:(which + 1) * size, :]
+
+    found = {}
+
+    def stage(i):
+        left, right = pl.ds(i * LANES, min(2, blocks - i) * LANES), slice(i * LANES, None)
+        total = None
+        for one, two in ((xm, xh), (xh, xm), (xh, xh)):
+            term = bdot(one[:, left], two[:, right], ((0,), (0,)))
+            total = term if total is None else total + term
+        for a in range(i, min(i + 2, blocks)):
+            for b in range(a, blocks):
+                found[a, b] = total[(a - i) * LANES:(a - i + 1) * LANES, (b - i) * LANES:(b - i + 1) * LANES]
+
+    def store(g):
+        names, start, size = groups[g]
+        for k, name in enumerate(names):
+            if name[0] != "pack":
+                value = found[name]
+            elif len(name) == 2:
+                value = found[name[1], name[1]]
+            else:
+                value = jnp.where(row <= col, found[name[1], name[1]], found[name[2], name[2]])
+            save(start + k * HALF, value)
+        if size > len(names) * HALF:
+            spare = size - len(names) * HALF
+            save(start + len(names) * HALF, jnp.zeros((2 * spare, LANES), jnp.float32))
+
+    def parcel(g):
+        if g < len(groups):
+            return groups[g][1], groups[g][2]
+        return tail, half - tail
+
+    def exchange(g):
+        low, size = parcel(g)
+        if g == len(groups) - 1:
+            size = half - low
+        return pltpu.make_async_remote_copy(
+            src_ref=part.at[pl.ds(pl.multiple_of((1 - core) * half + low, 8), size)],
+            dst_ref=swap.at[pl.ds(low, size)],
+            send_sem=swap_send.at[g], recv_sem=swap_recv.at[g],
+            device_id=where(me, 1 - core), device_id_type=MESH)
+
+    def absorb(g):
+        low, size = parcel(g)
+        if g == len(groups) - 1:
+            size = half - low
+        exchange(g).wait_recv()
+        acc[pl.ds(low, size), :] = (
+            part[pl.ds(pl.multiple_of(core * half + low, 8), size), :] + swap[pl.ds(low, size), :])
+
+    def each(g):
+        return parcel(g)[1] // np_ if g < len(groups) else half - tail
+
+    def spot(g, owner, base=0):
+        if g == len(groups):
+            return pl.ds(pl.multiple_of(base + tail, 8), each(g))
+        return pl.ds(pl.multiple_of(base + groups[g][1] + owner * each(g), 8), each(g))
+
+    def inbox(g):
+        return landed_tail if g == len(groups) else landed.at[g, :, pl.ds(0, each(g))]
+
+    def outbox(g):
+        return red_tail if g == len(groups) else red.at[g, pl.ds(0, each(g))]
+
+    def scatter(g, other):
+        return pltpu.make_async_remote_copy(
+            src_ref=acc.at[spot(g, other)], dst_ref=inbox(g).at[me],
+            send_sem=rs_send.at[g], recv_sem=rs_recv.at[g],
+            device_id=where(other, core), device_id_type=MESH)
+
+    def scatter_all(g):
+        others(np_, me, lambda other: scatter(g, other).start())
+
+    def scatter_wait(g, way):
+        copy = pltpu.make_async_remote_copy(
+            src_ref=inbox(g).at[pl.ds(0, np_ - 1)], dst_ref=inbox(g).at[pl.ds(0, np_ - 1)],
+            send_sem=rs_send.at[g], recv_sem=rs_recv.at[g],
+            device_id=where(me, core), device_id_type=MESH)
+        getattr(copy, way)()
+
+    base = core * half
+
+    def gather(g, other):
+        return pltpu.make_async_remote_copy(
+            src_ref=outbox(g), dst_ref=full.at[spot(g, me, base)],
+            send_sem=ag_send.at[g], recv_sem=ag_recv.at[g],
+            device_id=where(other, core), device_id_type=MESH)
+
+    def gather_wait(g, way):
+        copy = pltpu.make_async_remote_copy(
+            src_ref=inbox(g).at[pl.ds(0, np_ - 1)], dst_ref=inbox(g).at[pl.ds(0, np_ - 1)],
+            send_sem=ag_send.at[g], recv_sem=ag_recv.at[g],
+            device_id=where(me, core), device_id_type=MESH)
+        getattr(copy, way)()
+
+    def forward(g, origin):
+        low, size = parcel(g)
+        return pltpu.make_async_remote_copy(
+            src_ref=full.at[pl.ds(pl.multiple_of(origin + low, 8), size)],
+            dst_ref=full.at[pl.ds(pl.multiple_of(origin + low, 8), size)],
+            send_sem=fw_send.at[g], recv_sem=fw_recv.at[g],
+            device_id=where(me, 1 - core), device_id_type=MESH)
+
+    def total_of(g):
+        inbox(g)[me] = acc[spot(g, me), :]
+        outbox(g)[...] = lax.fori_loop(
+            1, np_, lambda k, total: total + inbox(g)[k], inbox(g)[0])
+        full[spot(g, me, base), :] = outbox(g)[...]
+
+    with jax.named_scope("stage0"):
+        stage(0)
+        store(0)
+    with jax.named_scope("bar"):
+        pl.semaphore_wait(barrier, ndev - 1)
+    exchange(0).start()
+    with jax.named_scope("stage1"):
+        for i in range(2, blocks, 2):
+            stage(i)
+        store(1)
+        extra = [jnp.sum(jnp.where(row == col, found[i, i], 0.0), axis=0, keepdims=True) for i in range(1, blocks, 2)]
+        extra.append(jnp.zeros((16 - len(extra), LANES), jnp.float32))
+        save(tail, jnp.concatenate(extra, axis=0))
+    exchange(1).start()
+    with jax.named_scope("absorb"):
+        absorb(0)
+        scatter_all(0)
+        absorb(1)
+        scatter_all(1)
+        @pl.when(me != center)
+        def _():
+            scatter(2, center).start()
+    for g in range(2):
+        with jax.named_scope(f"rs{g}"):
+            scatter_wait(g, "wait_recv")
+            total_of(g)
+            others(np_, me, lambda other: gather(g, other).start())
+
+    with jax.named_scope("rs2"):
+        @pl.when(me == center)
+        def _():
+            scatter_wait(2, "wait_recv")
+            total_of(2)
+            others(np_, me, lambda other: gather(2, other).start())
+    with jax.named_scope("ag0"):
+        gather_wait(0, "wait_recv")
+        forward(0, base).start()
+    with jax.named_scope("ag1"):
+        gather_wait(1, "wait_recv")
+        forward(1, base).start()
+    with jax.named_scope("ag2"):
+        @pl.when(me != center)
+        def _():
+            gather(2, me).wait_recv()
+        forward(2, base).start()
+    with jax.named_scope("drain"):
+        for g in range(2):
+            exchange(g).wait_send()
+            scatter_wait(g, "wait_send")
+            gather_wait(g, "wait_send")
+
+        @pl.when(me != center)
+        def _():
+            scatter(2, center).wait_send()
+
+        @pl.when(me == center)
+        def _():
+            gather_wait(2, "wait_send")
+    with jax.named_scope("fw"):
+        for g in range(3):
+            forward(g, half - base).wait_recv()
+
+    def block_at(start):
+        return jnp.concatenate([full[pl.ds(which * half + start, HALF), :] for which in range(2)], axis=0)
+
+    with jax.named_scope("coef"):
+        ends = jnp.concatenate([full[pl.ds(which * half + tail, 8), :] for which in range(2)], axis=0)
+        value = {}
+        for names, start, _ in groups:
+            for k, name in enumerate(names):
+                block = block_at(start + k * HALF) / count
+                if name[0] != "pack":
+                    value[name] = block
+                elif len(name) == 2:
+                    value[name[1], name[1]] = block
+                else:
+                    place = name[2] // 2
+                    flip = block.T
+                    value[name[1], name[1]] = jnp.where(row <= col, block, flip)
+                    diagonal = jnp.broadcast_to(ends[place:place + 1, :] / count, (LANES, LANES))
+                    value[name[2], name[2]] = jnp.where(row == col, diagonal, jnp.where(row > col, block, flip))
+        metric = jnp.concatenate([
+            jnp.concatenate([value[i, j] if i <= j else value[j, i].T for j in range(keep)], axis=1)
+            for i in range(keep)], axis=0)
+        first = jnp.concatenate([value[i, keep] for i in range(keep)], axis=0)
+        own = value[keep, keep]
+        split_metric = halves(metric)
+        once = dot3(split_metric, halves(first))
+        coef = first + (first - once)
+        split_coef = halves(coef)
+        twice = dot3(split_metric, split_coef)
+        rest = first + (first - twice)
+    with jax.named_scope("gramalg"):
+        a, b = split_coef
+        c, d = halves(rest)
+        one = bdot(a, jnp.concatenate([c, d], axis=1), ((0,), (0,)))
+        cross = one[:, :LANES] + (one[:, LANES:] + bdot(b, c, ((0,), (0,))))
+        gram = own - 0.5 * (cross + cross.T)
+    with jax.named_scope("guard"):
+        norm = jnp.sum(jnp.abs(metric), axis=0, keepdims=True)
+        norm = jnp.max(norm, axis=1, keepdims=True)
+        share = jnp.sum(jnp.where(row == col, own, 0.0), axis=0, keepdims=True) + jnp.sum(
+            jnp.abs(coef) * (2.0 * jnp.abs(first) + jnp.abs(twice)), axis=0, keepdims=True)
+        lengths = jnp.sum(first * first, axis=0, keepdims=True)
+        need = jnp.maximum(share * (1.0 / SHARE_LIMIT), norm * (2.0 + norm) * (2.0 + norm) * lengths * (1.0 / LENGTH_LIMIT))
+    with jax.named_scope("work"):
+        for start, size in ranges(rows, ROWS):
+            span = pl.ds(start, size)
+            work = held[span, :] - dot3((xh[span, :kept], xm[span, :kept]), split_coef)
+            high_out[span, :], low_out[span, :] = halves(work)
+    with jax.named_scope("factor"):
+        inverse, scales = inverse_factor(gram, 16)
+        last_out[...] = inverse.T
+        fine = jnp.logical_and(scales > 0.0, need * scales < 1.0)
+        good = jnp.where(jnp.logical_and(row == col, jnp.logical_not(fine)), 0.0, 1.0)
+        safe[0, 0] = jnp.min(good).astype(jnp.int32)
+    with jax.named_scope("drain2"):
+        for g in range(3):
+            forward(g, base).wait_send()
+
+
+def reduce_call(nx, ny, trial, resid, energy, shift):
+    rows, kept = trial.shape
+    new = resid.shape[1]
+    np_ = nx * (ny // 2)
+    groups, tail, half = plan(kept, new, np_)
+    most = max(size // np_ for _, _, size in groups)
+    f32, bf16 = jnp.float32, jnp.bfloat16
+    dma = pltpu.SemaphoreType.DMA
+    vmem = pl.BlockSpec(memory_space=pltpu.VMEM)
+    return pl.pallas_call(
+        functools.partial(reduce_kernel, nx, ny, float(rows * nx * ny)),
+        name="reduce",
+        out_shape=(
+            jax.ShapeDtypeStruct((rows, new), bf16), jax.ShapeDtypeStruct((rows, new), bf16),
+            jax.ShapeDtypeStruct((new, new), f32), jax.ShapeDtypeStruct((1, 1), jnp.int32)),
+        in_specs=[pl.BlockSpec(memory_space=pl.ANY)] * 2 + [vmem] * 2,
+        out_specs=(vmem, vmem, vmem, pl.BlockSpec(memory_space=pltpu.SMEM)),
+        scratch_shapes=[
+            pltpu.VMEM((rows, kept), f32),
+            *[pltpu.VMEM((rows, kept + new), bf16)] * 2,
+            pltpu.VMEM((rows, new), f32),
+            dma, dma,
+            pltpu.VMEM((2 * half, LANES), f32),
+            pltpu.VMEM((half, LANES), f32),
+            pltpu.VMEM((half, LANES), f32),
+            pltpu.VMEM((2, np_, most, LANES), f32),
+            pltpu.VMEM((np_, half - tail, LANES), f32),
+            pltpu.VMEM((2, most, LANES), f32),
+            pltpu.VMEM((half - tail, LANES), f32),
+            pltpu.VMEM((2 * half, LANES), f32),
+            dma((2,)), dma((2,)), dma((3,)), dma((3,)), dma((3,)), dma((3,)), dma((3,)), dma((3,)),
+        ],
         compiler_params=pltpu.CompilerParams(collective_id=0, has_side_effects=True),
-    )(trial, resid, energy.reshape(rows // LANES, LANES), shift.reshape(1, new))
+    )(trial, resid, energy, shift)
+
+
+def apply_kernel(high, low, last, basis, out, store):
+    rows = high.shape[0]
+    pieces = ranges(rows, 2 * ROWS)
+
+    def put(k):
+        start, size = pieces[k]
+        return pltpu.make_async_copy(out.at[pl.ds(start, size)], basis.at[pl.ds(start, size)], store.at[k])
+
+    right = halves(last[...])
+    for k, (start, size) in enumerate(pieces):
+        span = pl.ds(start, size)
+        out[span, :] = dot3((high[span, :], low[span, :]), right)
+        put(k).start()
+    for k in range(len(pieces)):
+        put(k).wait()
+
+
+def apply_call(high, low, last):
+    rows, new = high.shape
+    dma = pltpu.SemaphoreType.DMA
+    vmem = pl.BlockSpec(memory_space=pltpu.VMEM)
+    return pl.pallas_call(
+        apply_kernel,
+        name="apply",
+        out_shape=jax.ShapeDtypeStruct((rows, new), jnp.float32),
+        in_specs=[vmem, vmem, vmem],
+        out_specs=pl.BlockSpec(memory_space=pl.ANY),
+        scratch_shapes=[pltpu.VMEM((rows, new), jnp.float32), dma((len(ranges(rows, 2 * ROWS)),))],
+    )(high, low, last)
+
+
+def hand_on(values):
+    def body(source, target):
+        target[...] = source[...]
+    return pl.pallas_call(body, name="hand_on", out_shape=jax.ShapeDtypeStruct(values.shape, values.dtype))(values)
+
+
+def per_device(nx, ny, trial, resid, energy, shift):
+    rows, new = resid.shape
+    energy = energy.reshape(rows // LANES, LANES)
+    shift = shift.reshape(1, new)
+    high, low, last, safe = reduce_call(nx, ny, trial, resid, energy, shift)
+    return lax.cond(
+        safe[0, 0] > 0,
+        lambda: apply_call(high, low, last),
+        lambda: hand_on(robust_call(nx, ny, trial, resid, energy, shift)))
 
 
 def solution(mesh):

time: 50.7 us -> 35.5 us (0.70)
  the two profiles are of different devices: /device:TPU:0 before, /device:TPU:1 now
where the time goes in v1:
time: 35.5 us; the launch traced here: 35.4 us
  Pallas kernels  33.5 us (94%)
  local copies, waits for them, and re-layouts  0.89 us (3%)
  between operations  0.75 us (2%)
    pallas_call x1, Pallas kernels, reduce_call(): pl.pallas_call(functools.partial(reduce_kernel, nx, ny, float(rows * nx *...  31.6 us
    pallas_call x1, Pallas kernels, apply_call(): pl.pallas_call(apply_kernel, name='apply', out_shape=jax.ShapeDtypeStruct...  1.9 us
    unnamed x10, local copies, waits for them, and re-layouts  0.89 us

profile of v1, /device:TPU:1, one launch (start us, length us, event | category | flops | bytes accessed | tf_op | source)
XLA Modules:
  0.0 35.4 jit_solution(1818148319193618524)
XLA Ops:
  0.0 0.0 copy-start.1
  0.0 0.0 copy-start
  0.0 0.0 copy-start.4
  0.0 0.0 copy-start.3
  0.0 31.6 %reduce.1 = (bf16[1536,128]{1,0:T(8,128)(2,1)S(1)}, bf16[1536,128]{1,0:T(8,128)(2,1)}, f32[128,128]{1,0:T(8,128)}, s32[1,1]{1,0:T(1,128)}) custom-call(f32[1536,384]{1,0:T(8,128)} %trial.1, f32[1536,128]{1,0:T(8,128)} %resid.1, f32[12,128]{1,0:T(8,128)} %bitcast.3, f32[1,128]{1,0:T(1,128)} %bitcast.5), custom_call_target="tpu_custom_call" | custom-call | tf_op jit(solution)/shard_map/reduce/pallas_call | solution.py:728
  32.3 0.0 copy-done.1
  32.3 0.0 copy-done
  32.3 0.0 copy-done.4
  32.3 0.0 copy-done.3
  32.4 2.1 %conditional.1 = (f32[1536,128]{1,0:T(8,128)S(1)}) conditional(s32[]{:T(128)} %bitcast.2, (f32[1536,384]{1,0:T(8,128)S(1)}, f32[1536,128]{1,0:T(8,128)S(1)}, f32[12,128]{1,0:T(8,128)S(1)}, f32[1,128]{1,0:T(1,128)S(1)}) %tuple.21, (bf16[1536,128]{1,0:T(8,128)(2,1)S(1)}, bf16[1536,128]{1,0:T(8,128)(2,1)}, f32[128,128]{1,0:T(8,128)}) %tuple.12), branch_computations={%region_0.0_spmd, %region_1.0_spmd} | conditional | bytes 8 | solution.py:797
  32.6 1.9 %apply.1 = f32[1536,128]{1,0:T(8,128)S(1)} custom-call(bf16[1536,128]{1,0:T(8,128)(2,1)S(1)} %get-tuple-element.26.high, bf16[1536,128]{1,0:T(8,128)(2,1)} %get-tuple-element.27.low, f32[128,128]{1,0:T(8,128)} %get-tuple-element.28.last), custom_call_target="tpu_custom_call" | custom-call | tf_op jit(solution)/shard_map/cond/branch_1_fun/apply/pallas_call | solution.py:776
  34.5 0.0 copy-start.2
  34.5 0.9 %copy-done.2 = f32[1536,128]{1,0:T(8,128)} copy-done((f32[1536,128]{1,0:T(8,128)}, f32[1536,128]{1,0:T(8,128)S(1)}, u32[]{:S(2)}) %copy-start.2) | copy-done | bytes 786456
Async XLA Ops:
  0.0 32.3 %copy-start.1 = (f32[1536,128]{1,0:T(8,128)S(1)}, f32[1536,128]{1,0:T(8,128)}, u32[]{:S(2)}) copy-start(f32[1536,128]{1,0:T(8,128)} %resid.1) | copy-start | bytes 2359300
  0.0 32.3 %copy-start = (f32[1536,384]{1,0:T(8,128)S(1)}, f32[1536,384]{1,0:T(8,128)}, u32[]{:S(2)}) copy-start(f32[1536,384]{1,0:T(8,128)} %trial.1) | copy-start | bytes 7077892
  0.0 32.3 %copy-start.4 = (f32[128]{0:T(128)S(1)}, f32[128]{0:T(128)}, u32[]{:S(2)}) copy-start(f32[128]{0:T(128)} %param.9) | copy-start | bytes 1540
  0.0 32.3 %copy-start.3 = (f32[1536]{0:T(1024)S(1)}, f32[1536]{0:T(1024)}, u32[]{:S(2)}) copy-start(f32[1536]{0:T(1024)} %param.8) | copy-start | bytes 18436
  34.5 0.9 %copy-start.2 = (f32[1536,128]{1,0:T(8,128)}, f32[1536,128]{1,0:T(8,128)S(1)}, u32[]{:S(2)}) copy-start(f32[1536,128]{1,0:T(8,128)S(1)} %get-tuple-element.40) | copy-start | bytes 2359300
